TPU v7x, 32 devices: a whole 2x2x4 slice. The times are simulated.
32 devices in a mesh: dp: 8 (over z, y), tensor: 4 (over x, core).
Axes of the slice: x: 2, y: 2, z: 4, core: 2. Of those that a mesh axis runs over, the one named last changes fastest.
Arguments:
- tokens: bfloat16 [12288, 1024], P('dp', 'tensor'), may hold values from -6 to 6
- segment_ids: int32 [12288], P('dp'), may hold values from 0 to 8, as said below
- w_query: bfloat16 [1024, 1024], P(None, 'tensor'), may hold values from -0.1875 to 0.1875
- w_key: bfloat16 [1024, 1024], P(None, 'tensor'), may hold values from -0.1875 to 0.1875
- w_value: bfloat16 [1024, 1024], P(None, 'tensor'), may hold values from -0.1875 to 0.1875
- b_query: bfloat16 [1024], P('tensor'), may hold values from -3 to 3
- b_value: bfloat16 [1024], P('tensor'), may hold values from -3 to 3
- w_out: bfloat16 [1024, 1024], P('tensor'), may hold values from -0.75 to 0.75
- b_out: bfloat16 [1024], P('tensor'), may hold values from -3 to 3
- gain_one: bfloat16 [1024], P('tensor'), may hold values from 0.5 to 1.5
- bias_one: bfloat16 [1024], P('tensor'), may hold values from -3 to 3
- w_in: bfloat16 [1024, 4096], P(None, 'tensor'), may hold values from -0.1875 to 0.1875
- b_in: bfloat16 [4096], P('tensor'), may hold values from -3 to 3
- w_down: bfloat16 [4096, 1024], P('tensor'), may hold values from -0.09375 to 0.09375
- b_down: bfloat16 [1024], P('tensor'), may hold values from -3 to 3
- gain_two: bfloat16 [1024], P('tensor'), may hold values from 0.5 to 1.5
- bias_two: bfloat16 [1024], P('tensor'), may hold values from -3 to 3
- cotangent: bfloat16 [12288, 1024], P('dp', 'tensor'), may hold values from -6 to 6
Outputs:
- out: bfloat16 [12288, 1024], P('dp', 'tensor')
- grad_tokens: bfloat16 [12288, 1024], P('dp', 'tensor')
- grad_w_query: float32 [1024, 1024], P(None, 'tensor')
- grad_w_key: float32 [1024, 1024], P(None, 'tensor')
- grad_w_value: float32 [1024, 1024], P(None, 'tensor')
- grad_b_query: float32 [1024], P('tensor')
- grad_b_value: float32 [1024], P('tensor')
- grad_w_out: float32 [1024, 1024], P('tensor')
- grad_b_out: float32 [1024], P('tensor')
- grad_gain_one: float32 [1024], P('tensor')
- grad_bias_one: float32 [1024], P('tensor')
- grad_w_in: float32 [1024, 4096], P(None, 'tensor')
- grad_b_in: float32 [4096], P('tensor')
- grad_w_down: float32 [4096, 1024], P('tensor')
- grad_b_down: float32 [1024], P('tensor')
- grad_gain_two: float32 [1024], P('tensor')
- grad_bias_two: float32 [1024], P('tensor')
Inputs may be any that keep to these rules, and one draw needn't show every extreme that they name: `segment_ids`: within each packed sequence of 512 tokens the ids run from 1 to 8 without falling, each id on at least one token, followed by one or more tail slots of id 0.
All inputs are finite; a program needn't handle non-finite values.
Results may differ from a plain program's by a relative error of at most 0.015.
Values may be sent and summed in bfloat16 or wider, within the bound.
No kernel may reach another device: no remote copies, remote signals or barrier semaphores. Data moves between devices by JAX's collectives and lax.ppermute only.
A program may use at most 128 MiB of HBM per device.

v0:
```python
import jax
import jax.numpy as jnp
from jax import lax
from jax.sharding import PartitionSpec as P

HD = 64
LEN = 512
epsilon = 1e-05
masked_fill = -1000000000.0


def over_rows(left, right):
    return lax.dot_general(
        left, right, (((0,), (0,)), ((), ())), preferred_element_type=jnp.float32
    )


def against(left, right):
    return lax.dot_general(
        left, right, (((1,), (1,)), ((), ())), preferred_element_type=jnp.float32
    )


def allowed_pairs(labels):
    length = labels.shape[0]
    same_label = labels[:, None] == labels[None, :]
    diagonal = lax.broadcasted_iota(jnp.int32, (length, length), 0) == lax.broadcasted_iota(
        jnp.int32, (length, length), 1
    )
    return same_label & ((labels[:, None] != 0) | diagonal)


def masked_scores(query_rows, key_rows, labels):
    score_scale = query_rows.shape[-1] ** (-0.5)
    scores = (
        jnp.einsum("qhd,khd->hqk", query_rows, key_rows, preferred_element_type=jnp.float32)
        * score_scale
    )
    return (jnp.where(allowed_pairs(labels)[None], scores, masked_fill), score_scale)


def attend_block(sliced):
    query_rows, key_rows, value_rows, labels = sliced
    scores, score_scale = masked_scores(query_rows, key_rows, labels)
    row_peak = jnp.max(scores, axis=-1, keepdims=True)
    exp_terms = jnp.exp(scores - row_peak)
    exp_total = jnp.sum(exp_terms, axis=-1, keepdims=True)
    probs = (exp_terms / exp_total).astype(jnp.bfloat16)
    context = jnp.einsum("hqk,khd->qhd", probs, value_rows, preferred_element_type=jnp.float32)
    return (context.astype(jnp.bfloat16), (row_peak + jnp.log(exp_total))[..., 0])


def attend_back(sliced):
    query_rows, key_rows, value_rows, labels, dcontext, log_total = sliced
    scores, score_scale = masked_scores(query_rows, key_rows, labels)
    probs = jnp.exp(scores - log_total[..., None])
    dprobs = jnp.einsum("qhd,khd->hqk", dcontext, value_rows, preferred_element_type=jnp.float32)
    row_delta = jnp.sum(probs * dprobs, axis=-1, keepdims=True)
    dscores = (probs * (dprobs - row_delta)).astype(jnp.bfloat16)
    dquery = (
        jnp.einsum("hqk,khd->qhd", dscores, key_rows, preferred_element_type=jnp.float32)
        * score_scale
    )
    dkey = (
        jnp.einsum("hqk,qhd->khd", dscores, query_rows, preferred_element_type=jnp.float32)
        * score_scale
    )
    dvalue = jnp.einsum(
        "hqk,qhd->khd", probs.astype(jnp.bfloat16), dcontext, preferred_element_type=jnp.float32
    )
    return (dquery.astype(jnp.bfloat16), dkey.astype(jnp.bfloat16), dvalue.astype(jnp.bfloat16))


def norm_from(values, row_sums, model_width):
    row_mean = row_sums[0] / model_width
    variance = row_sums[1] / model_width - row_mean * row_mean
    inv_std = lax.rsqrt(variance + epsilon)
    return ((values - row_mean[:, None]) * inv_std[:, None], inv_std)


def norm_back(scaled, normed, inv_std, row_sums, model_width):
    return inv_std[:, None] * (
        scaled - row_sums[0][:, None] / model_width - normed * row_sums[1][:, None] / model_width
    )


def summed(parts):
    return lax.psum(parts, "dp")


def local(
    tokens,
    segment_ids,
    w_query,
    w_key,
    w_value,
    b_query,
    b_value,
    w_out,
    b_out,
    gain_one,
    bias_one,
    w_in,
    b_in,
    w_down,
    b_down,
    gain_two,
    bias_two,
    cotangent,
):
    row_count = tokens.shape[0]
    model_width = w_query.shape[0]
    local_cols = w_query.shape[1]
    head_count = local_cols // HD
    seq_count = row_count // LEN
    proj_weight = jnp.concatenate([w_query, w_key, w_value], axis=1)
    proj_bias = jnp.concatenate(
        [
            b_query.astype(jnp.float32),
            jnp.zeros((local_cols,), jnp.float32),
            b_value.astype(jnp.float32),
        ]
    )
    inputs = lax.all_gather(tokens, "tensor", axis=1, tiled=True)
    projected = (
        jnp.dot(inputs, proj_weight, preferred_element_type=jnp.float32) + proj_bias
    ).astype(jnp.bfloat16)

    def heads_of(block):
        return block.reshape(seq_count, LEN, head_count, HD)

    queries = heads_of(projected[:, :local_cols])
    key_proj = heads_of(projected[:, local_cols : 2 * local_cols])
    value_proj = heads_of(projected[:, 2 * local_cols :])
    labels = segment_ids.reshape(seq_count, LEN)
    context, log_total = lax.map(attend_block, (queries, key_proj, value_proj, labels))
    context = context.reshape(row_count, local_cols)
    attn_mine = lax.psum_scatter(
        jnp.dot(context, w_out, preferred_element_type=jnp.float32),
        "tensor",
        scatter_dimension=1,
        tiled=True,
    )
    z_one = tokens.astype(jnp.float32) + attn_mine + b_out.astype(jnp.float32)
    sums_one = lax.psum((jnp.sum(z_one, axis=1), jnp.sum(z_one * z_one, axis=1)), "tensor")
    n_one, inv_one = norm_from(z_one, sums_one, model_width)
    h_one = n_one * gain_one.astype(jnp.float32) + bias_one.astype(jnp.float32)
    h_low = lax.all_gather(h_one.astype(jnp.bfloat16), "tensor", axis=1, tiled=True)
    pre_act = jnp.dot(h_low, w_in, preferred_element_type=jnp.float32) + b_in.astype(jnp.float32)
    hidden = jax.nn.gelu(pre_act, approximate=False).astype(jnp.bfloat16)
    feed_mine = lax.psum_scatter(
        jnp.dot(hidden, w_down, preferred_element_type=jnp.float32),
        "tensor",
        scatter_dimension=1,
        tiled=True,
    )
    z_two = h_one + feed_mine + b_down.astype(jnp.float32)
    sums_two = lax.psum((jnp.sum(z_two, axis=1), jnp.sum(z_two * z_two, axis=1)), "tensor")
    n_two, inv_two = norm_from(z_two, sums_two, model_width)
    result = (n_two * gain_two.astype(jnp.float32) + bias_two.astype(jnp.float32)).astype(
        jnp.bfloat16
    )
    grad_out = cotangent.astype(jnp.float32)
    grad_gain_two = jnp.sum(grad_out * n_two, axis=0)
    grad_bias_two = jnp.sum(grad_out, axis=0)
    scaled_two = grad_out * gain_two.astype(jnp.float32)
    back_two = lax.psum(
        (jnp.sum(scaled_two, axis=1), jnp.sum(scaled_two * n_two, axis=1)), "tensor"
    )
    dz_two = norm_back(scaled_two, n_two, inv_two, back_two, model_width)
    grad_b_down = jnp.sum(dz_two, axis=0)
    dz_two_low = lax.all_gather(dz_two.astype(jnp.bfloat16), "tensor", axis=1, tiled=True)
    grad_w_down = over_rows(hidden, dz_two_low)
    dhidden = against(dz_two_low, w_down)
    _, gelu_pull = jax.vjp(lambda value_in: jax.nn.gelu(value_in, approximate=False), pre_act)
    dpre = gelu_pull(dhidden)[0].astype(jnp.bfloat16)
    grad_w_in = over_rows(h_low, dpre)
    grad_b_in = jnp.sum(dpre.astype(jnp.float32), axis=0)
    dh_one = dz_two + lax.psum_scatter(
        against(dpre, w_in), "tensor", scatter_dimension=1, tiled=True
    )
    feed_grads = (grad_w_in, grad_b_in, grad_w_down, grad_b_down, grad_gain_two, grad_bias_two)
    grad_gain_one = jnp.sum(dh_one * n_one, axis=0)
    grad_bias_one = jnp.sum(dh_one, axis=0)
    scaled_one = dh_one * gain_one.astype(jnp.float32)
    back_one = lax.psum(
        (jnp.sum(scaled_one, axis=1), jnp.sum(scaled_one * n_one, axis=1)), "tensor"
    )
    dz_one = norm_back(scaled_one, n_one, inv_one, back_one, model_width)
    grad_b_out = jnp.sum(dz_one, axis=0)
    dz_one_low = lax.all_gather(dz_one.astype(jnp.bfloat16), "tensor", axis=1, tiled=True)
    grad_w_out = over_rows(context, dz_one_low)
    dcontext = heads_of(against(dz_one_low, w_out).astype(jnp.bfloat16))
    dquery, dkey, dvalue = lax.map(
        attend_back, (queries, key_proj, value_proj, labels, dcontext, log_total)
    )
    dprojected = jnp.concatenate(
        [
            dquery.reshape(row_count, local_cols),
            dkey.reshape(row_count, local_cols),
            dvalue.reshape(row_count, local_cols),
        ],
        axis=1,
    )
    grad_proj = over_rows(inputs, dprojected)
    grad_b_query = jnp.sum(dprojected[:, :local_cols].astype(jnp.float32), axis=0)
    grad_b_value = jnp.sum(dprojected[:, 2 * local_cols :].astype(jnp.float32), axis=0)
    input_part = lax.psum_scatter(
        against(dprojected, proj_weight).astype(jnp.bfloat16),
        "tensor",
        scatter_dimension=1,
        tiled=True,
    ).astype(jnp.float32)
    grad_tokens = (dz_one + input_part).astype(jnp.bfloat16)
    attention_grads = (
        grad_proj[:, :local_cols],
        grad_proj[:, local_cols : 2 * local_cols],
        grad_proj[:, 2 * local_cols :],
        grad_b_query,
        grad_b_value,
        grad_w_out,
        grad_b_out,
        grad_gain_one,
        grad_bias_one,
    )
    totals = tuple(summed(attention_grads + feed_grads))
    return (result, grad_tokens) + totals


def solution(mesh):
    placed = (
        P("dp", "tensor"),
        P("dp"),
        P(None, "tensor"),
        P(None, "tensor"),
        P(None, "tensor"),
        P("tensor"),
        P("tensor"),
        P("tensor", None),
        P("tensor"),
        P("tensor"),
        P("tensor"),
        P(None, "tensor"),
        P("tensor"),
        P("tensor", None),
        P("tensor"),
        P("tensor"),
        P("tensor"),
        P("dp", "tensor"),
    )
    return jax.shard_map(
        local,
        mesh=mesh,
        in_specs=placed,
        out_specs=(
            P("dp", "tensor"),
            P("dp", "tensor"),
            P(None, "tensor"),
            P(None, "tensor"),
            P(None, "tensor"),
            P("tensor"),
            P("tensor"),
            P("tensor", None),
            P("tensor"),
            P("tensor"),
            P("tensor"),
            P(None, "tensor"),
            P("tensor"),
            P("tensor", None),
            P("tensor"),
            P("tensor"),
            P("tensor"),
        ),
        check_vma=False,
    )
```

profile of v0, /device:TPU:0, one launch (start us, length us, event | category | flops | bytes accessed | tf_op | source)
XLA Modules:
  0.0 971.1 jit_solution(15447300485332187335)
XLA Ops:
  14.6 26.6 %all-gather.5.cloned.1.call-done = bf16[1536,1024]{1,0:T(8,128)(2,1)} async-done(((bf16[1536,256]{1,0:T(8,128)(2,1)}), bf16[1536,1024]{1,0:T(8,128)(2,1)}) %all-gather.5.cloned.1.call-update) | async-done | bytes 3145744 | tf_op jit(solution)/shard_map/all_gather | solution.py:124
  41.2 5.2 fusion.69
  50.4 3.6 reshape.227
  54.0 2.3 copy.54
  56.3 3.6 reshape.225
  59.9 2.3 copy.53
  63.1 18.4 %while.26 = (s32[]{:T(128)}, bf16[3,512,4,64]{1,3,2,0:T(8,128)(2,1)}, f32[3,4,512]{2,1,0:T(4,128)S(1)}, bf16[3,512,4,64]{1,3,2,0:T(8,128)(2,1)}, s32[3,512]{1,0:...) while((s32[]{:T(128)}, ...), condition=%wide.region_3.4_spmd, body=%wide.region_0.3_spmd.sunk | while | flops 282196480 | bytes 14756965 | solution.py:136
  66.2 3.0 fusion.140
  72.3 3.0 fusion.140
  78.4 3.0 fusion.140
  84.5 3.7 fusion.86
  88.9 57.4 %reduce-scatter.5.cloned.1.call-done = f32[1536,256]{1,0:T(8,128)} async-done(((f32[1536,1024]{1,0:T(8,128)}), f32[1536,256]{1,0:T(8,128)}) %reduce-scatter.5.cloned.1.call-update) | async-done | bytes 1572880 | tf_op jit(solution)/shard_map/reduce_scatter | solution.py:138
  146.3 3.0 fusion.79
  149.3 10.4 %all-reduce.5 = (f32[1536]{0:T(1024)S(1)}, f32[1536]{0:T(1024)S(1)}) all-reduce(f32[1536]{0:T(1024)S(1)} %get-tuple-element.191, f32[1536]{0:T(1024)S(1)} %get-tuple-element.190), channel_id=1, replica_groups=mesh['dp'=8,'tensor'=4] {'tensor'}, use_global_device_ids=true, to_apply=%region_8.9 | all-reduce | flops 3072 | bytes 24576 | tf_op jit(solution)/shard_map/psum | solution.py:145
  159.6 2.8 fusion.77
  162.5 29.6 %all-gather.7.cloned.1.call-done = bf16[1536,1024]{1,0:T(8,128)(2,1)} async-done(((bf16[1536,256]{1,0:T(8,128)(2,1)}), bf16[1536,1024]{1,0:T(8,128)(2,1)}) %all-gather.7.cloned.1.call-update) | async-done | bytes 3145744 | tf_op jit(solution)/shard_map/all_gather | solution.py:148
  192.1 19.5 %multiply_convert_fusion.1 = (bf16[1536,1024]{1,0:T(8,128)(2,1)S(1)}, f32[1536,1024]{1,0:T(8,128)}, f32[1536,1024]{1,0:T(8,128)}) fusion(f32[1024]{0:T(1024)S(1)} %convert_element_type.124, bf16[1536,1024]{1,0:T(8,128)(2,1)} %all-gather.7.cloned.1.call-done, bf16[1024,1024]{1,0:T(8,128)(2,1)S(1)} %copy-done), kind=kOutput, calls=%fused_computation.76 | convolution fusion | flops 3325034496 | bytes 20975616 | tf_op jit(solution)/shard_map/dot_general | solution.py:149
  213.4 5.3 fusion.87
  219.4 57.4 %reduce-scatter.7.cloned.1.call-done = f32[1536,256]{1,0:T(8,128)} async-done(((f32[1536,1024]{1,0:T(8,128)}), f32[1536,256]{1,0:T(8,128)}) %reduce-scatter.7.cloned.1.call-update) | async-done | bytes 1572880 | tf_op jit(solution)/shard_map/reduce_scatter | solution.py:151
  276.7 3.5 fusion.78
  280.3 10.1 %all-reduce.4 = (f32[1536]{0:T(1024)S(1)}, f32[1536]{0:T(1024)S(1)}) all-reduce(f32[1536]{0:T(1024)S(1)} %get-tuple-element.189, f32[1536]{0:T(1024)S(1)} %get-tuple-element.188), channel_id=1, replica_groups=mesh['dp'=8,'tensor'=4] {'tensor'}, use_global_device_ids=true, to_apply=%region_13.14 | all-reduce | flops 3072 | bytes 24576 | tf_op jit(solution)/shard_map/psum | solution.py:158
  290.4 2.6 fusion.76
  293.0 10.1 %all-reduce.3 = (f32[1536]{0:T(1024)S(1)}, f32[1536]{0:T(1024)S(1)}) all-reduce(f32[1536]{0:T(1024)S(1)} %get-tuple-element.185, f32[1536]{0:T(1024)S(1)} %get-tuple-element.192), channel_id=1, replica_groups=mesh['dp'=8,'tensor'=4] {'tensor'}, use_global_device_ids=true, to_apply=%region_17.18 | all-reduce | flops 3072 | bytes 24576 | tf_op jit(solution)/shard_map/psum | solution.py:167
  303.2 3.1 fusion.80
  308.7 29.4 %all-gather.9.cloned.1.call-done = bf16[1536,1024]{1,0:T(8,128)(2,1)} async-done(((bf16[1536,256]{1,0:T(8,128)(2,1)}), bf16[1536,1024]{1,0:T(8,128)(2,1)}) %all-gather.9.cloned.1.call-update) | async-done | bytes 3145744 | tf_op jit(solution)/shard_map/all_gather | solution.py:172
  338.1 11.8 %convert_reduce_fusion = (f32[1024]{0:T(1024)S(1)}, bf16[1536,1024]{1,0:T(8,128)(2,1)S(1)}) fusion(f32[1536,1024]{1,0:T(8,128)} %get-tuple-element.260, f32[1536,1024]{1,0:T(8,128)} %get-tuple-element.277, f32[1024]{0:T(1024)S(1)} %convert_element_type.124, bf16[1536,1024]{1,0:T(8,128)(2,1)} %all-gather.9.cloned.1.call-done, bf16[1024,1024]{1,0:T(8,128)(2,1)} %param.35), kind=kOutput, calls=%fused_computation.74 | convolution fusion | flops 3247963136 | bytes 20979712 | tf_op jit(solution)/shard_map/dot_general | solution.py:19
  351.6 5.6 fusion.88
  357.2 58.0 %reduce-scatter.9.cloned.1.call-done = f32[1536,256]{1,0:T(8,128)} async-done(((f32[1536,1024]{1,0:T(8,128)}), f32[1536,256]{1,0:T(8,128)}) %reduce-scatter.9.cloned.1.call-update) | async-done | bytes 1572880 | tf_op jit(solution)/shard_map/reduce_scatter | solution.py:179
  415.2 3.4 multiply_reduce_fusion.1
  418.6 10.1 %all-reduce.2 = (f32[1536]{0:T(1024)S(1)}, f32[1536]{0:T(1024)S(1)}) all-reduce(f32[1536]{0:T(1024)S(1)} %get-tuple-element.183, f32[1536]{0:T(1024)S(1)} %get-tuple-element.186), channel_id=1, replica_groups=mesh['dp'=8,'tensor'=4] {'tensor'}, use_global_device_ids=true, to_apply=%region_22.23 | all-reduce | flops 3072 | bytes 24576 | tf_op jit(solution)/shard_map/psum | solution.py:186
  428.8 2.3 fusion.82
  433.7 29.2 %all-gather.11.cloned.1.call-done = bf16[1536,1024]{1,0:T(8,128)(2,1)} async-done(((bf16[1536,256]{1,0:T(8,128)(2,1)}), bf16[1536,1024]{1,0:T(8,128)(2,1)}) %all-gather.11.cloned.1.call-update) | async-done | bytes 3145744 | tf_op jit(solution)/shard_map/all_gather | solution.py:191
  462.9 2.9 convolution_convert_fusion.1
  467.4 3.4 copy.60
  472.7 26.4 %while.27 = (s32[]{:T(128)}, bf16[3,512,4,64]{1,3,2,0:T(8,128)(2,1)}, bf16[3,512,4,64]{1,3,2,0:T(8,128)(2,1)}, bf16[3,512,4,64]{1,3,2,0:T(8,128)(2,1)S(1)}, bf16...) while((s32[]{:T(128)}, ...), condition=%wide.region_25.26_spmd, body=%wide.region_23.25_spmd.sunk | while | flops 688519680 | bytes 38344856 | solution.py:194
  475.1 2.5 multiply_reduce_fusion.7
  483.9 2.5 multiply_reduce_fusion.7
  492.7 2.5 multiply_reduce_fusion.7
  504.9 5.5 convolution_convert_fusion
  510.6 8.6 fusion.91
  519.3 5.0 fusion.90
  524.3 2.6 convolution_bitcast_fusion
  534.9 37.7 %all-reduce = (f32[256]{0:T(256)}, f32[256]{0:T(256)}, f32[256]{0:T(256)}, f32[256]{0:T(256)}, f32[256]{0:T(256)}, /*index=5*/f32[1024]{0:T(1024)}, f32[256]{0:T(256)}, f32[256]{0:T(256)}, f32[256]{0:T(256)}) all-reduce(f32[256]{0:T(256)S(1)} %reduce_sum.184, f32[256]{0:T(256)S(1)} %reduce_sum.186, ...), channel_id=1, replica_groups=mesh['dp'=8,'tensor'=4] {'dp'}, use_global_device_ids=true, to_apply=%region_31.32 | all-reduce | flops 3072 | bytes 24576 | tf_op jit(solution)/shard_map/psum | solution.py:88
  572.7 2.2 add_convert_fusion.2
  574.9 375.0 %all-reduce.8.cloned.1.call-done = (f32[1024,256]{0,1:T(8,128)}, f32[1024,256]{0,1:T(8,128)}, f32[1024,256]{0,1:T(8,128)}, f32[256,1024]{1,0:T(8,128)}, f32[1024,1024]{1,0:T(8,128)}, /*index=5*/f32[1024,1024]{1,0:T(8,128)}) async-done(((f32[1024,256]{0,1:T(8,128)}, f32[1024,256]{0,1:T(8,128)}, f32[1024,256]{0,1:T(8,128)}, f32[256,1024]{1,0:T(8,128)}, f32[1024,1024]{1,0:T(8,128)}, ...) | async-done | bytes 12582928 | tf_op jit(solution)/shard_map/psum | solution.py:88
  949.9 2.7 copy.65
  952.6 2.5 copy.66
  957.4 4.9 copy.117
  (185 shorter events, 75.0 us)
Async XLA Ops:
  7.2 184.9 %copy-start = (bf16[1024,1024]{1,0:T(8,128)(2,1)S(1)}, bf16[1024,1024]{1,0:T(8,128)(2,1)}, u32[]{:S(2)}) copy-start(bf16[1024,1024]{1,0:T(8,128)(2,1)} %param.33) | copy-start | bytes 6291460
  7.2 6.6 copy-start.17
  7.2 34.0 %all-gather.5.cloned.1.call-start = ((), (), s32[]{:S(2)}) async-start(), calls=%async_computation.4 | async-start | bytes 3932160 | tf_op jit(solution)/shard_map/all_gather | solution.py:124
  8.0 138.3 %reduce-scatter.5.cloned.1.call-start = ((), (), s32[]{:S(2)}) async-start(), calls=%async_computation.5 | async-start | bytes 7864320 | tf_op jit(solution)/shard_map/reduce_scatter | solution.py:138
  81.5 3.0 copy-start.16
  83.6 0.9 copy-start.10
  88.2 0.7 copy-start.25
  88.2 0.7 copy-start.26
  88.2 0.7 copy-start.27
  88.2 103.9 %all-gather.7.cloned.1.call-start = ((), (), s32[]{:S(2)}) async-start(), calls=%async_computation.6 | async-start | bytes 3932160 | tf_op jit(solution)/shard_map/all_gather | solution.py:148
  88.9 73.6 %copy-start.20 = (bf16[1024]{0:T(1024)(128)(2,1)S(1)}, bf16[1024]{0:T(1024)(128)(2,1)}, u32[]{:S(2)}) copy-start(bf16[1024]{0:T(1024)(128)(2,1)} %param.34) | copy-start | bytes 6148
  162.4 114.3 %reduce-scatter.7.cloned.1.call-start = ((), (), s32[]{:S(2)}) async-start(), calls=%async_computation.7 | async-start | bytes 7864320 | tf_op jit(solution)/shard_map/reduce_scatter | solution.py:151
  192.1 21.3 %copy-start.24 = (bf16[1024,1024]{1,0:T(8,128)(2,1)S(1)}, bf16[1024,1024]{1,0:T(8,128)(2,1)}, u32[]{:S(2)}) copy-start(bf16[1024,1024]{1,0:T(8,128)(2,1)} %param.35) | copy-start | bytes 6291460
  211.6 1.8 copy-start.31
  218.7 0.7 copy-start.28
  218.7 0.7 copy-start.29
  218.7 0.7 copy-start.30
  218.7 119.4 %all-gather.9.cloned.1.call-start = ((), (), s32[]{:S(2)}) async-start(), calls=%async_computation.8 | async-start | bytes 3932160 | tf_op jit(solution)/shard_map/all_gather | solution.py:172
  306.3 1.1 copy-start.6
  308.4 106.8 %reduce-scatter.9.cloned.1.call-start = ((), (), s32[]{:S(2)}) async-start(), calls=%async_computation.9 | async-start | bytes 7864320 | tf_op jit(solution)/shard_map/reduce_scatter | solution.py:179
  349.9 1.7 copy-start.32
  357.1 58.0 %copy-start.2 = (f32[1536,256]{1,0:T(8,128)S(1)}, f32[1536,256]{1,0:T(8,128)}, u32[]{:S(2)}) copy-start(f32[1536,256]{1,0:T(8,128)} %get-tuple-element.261) | copy-start | bytes 4718596
  357.2 105.7 %all-gather.11.cloned.1.call-start = ((), (), s32[]{:S(2)}) async-start(), calls=%async_computation.10 | async-start | bytes 3932160 | tf_op jit(solution)/shard_map/all_gather | solution.py:191
  431.0 1.2 copy-start.4
  433.2 139.4 %reduce-scatter.11.cloned.1.call-start = ((), (), s32[]{:S(2)}) async-start(), calls=%async_computation.11 | async-start | bytes 3932160 | tf_op jit(solution)/shard_map/reduce_scatter | solution.py:208
  465.8 6.9 copy-start.3
  472.7 1.1 copy-start.9
  481.5 1.1 copy-start.9
  490.3 1.1 copy-start.9
  499.1 3.2 copy-start.7
  501.2 1.2 copy-start.13
  503.4 1.4 copy-start.18
  510.4 439.5 %all-reduce.8.cloned.1.call-start = ((), (), s32[]{:S(2)}) async-start(), calls=%async_computation.12 | async-start | bytes 25165824 | tf_op jit(solution)/shard_map/psum | solution.py:88
  510.6 8.7 copy-start.22
  510.6 8.7 copy-start.33
  519.3 5.0 copy-start.19
  519.3 5.0 copy-start.21
  526.9 1.8 copy-start.11
  526.9 3.3 copy-start.23
  532.2 1.1 copy-start.8
  532.2 40.4 %copy-start.5 = (f32[1536,256]{1,0:T(8,128)S(1)}, f32[1536,256]{1,0:T(8,128)}, u32[]{:S(2)}) copy-start(f32[1536,256]{1,0:T(8,128)} %copy-done.4) | copy-start | bytes 4718596
  949.9 5.2 copy-start.15
  949.9 6.5 copy-start.14
  957.4 4.9 copy-start.12
  957.4 7.0 copy-start.1
Sparse Core Ops, SparseCore 0:
  9.6 31.6 all-gather.4
  88.4 57.8 reduce-scatter.4
  162.5 29.5 all-gather.6
  218.8 57.8 reduce-scatter.6
  308.5 29.4 all-gather.8
  357.3 57.8 reduce-scatter.8
  433.4 29.4 all-gather.10
  510.5 37.7 reduce-scatter.10
  554.8 395.0 all-reduce.7
where the time goes:
time: 981 us; the launch traced here: 971 us
  waiting for transfers between devices  663 us (68%)
  matrix products  114 us (12%)
  blocking collectives  78.5 us (8%)
  local copies, waits for them, and re-layouts  63.9 us (7%)
  other arithmetic  35.8 us (4%)
  between operations  14.4 us (1%)
    psum x1, waiting for transfers between devices, summed(): return lax.psum(parts, 'dp')  375 us
    reduce_scatter x1, waiting for transfers between devices, local(): lax.psum_scatter(against(dpre, w_in), 'tensor', scatter_dimension=1, tile...  58 us
    reduce_scatter x1, waiting for transfers between devices, local(): lax.psum_scatter(jnp.dot(hidden, w_down, preferred_element_type=jnp.float...  57.4 us
    reduce_scatter x1, waiting for transfers between devices, local(): lax.psum_scatter(jnp.dot(context, w_out, preferred_element_type=jnp.float...  57.4 us
    psum x1, blocking collectives, summed(): return lax.psum(parts, 'dp')  37.7 us
    unnamed x80, local copies, waits for them, and re-layouts  31.2 us
    all_gather x1, waiting for transfers between devices, local(): lax.all_gather(h_one.astype(jnp.bfloat16), 'tensor', axis=1, tiled=True)  29.6 us
    all_gather x1, waiting for transfers between devices, local(): lax.all_gather(dz_two.astype(jnp.bfloat16), 'tensor', axis=1, tiled=True)  29.4 us
  transfers between devices with their start and end apart: 9, of which 8 were waited for; matrix products, arithmetic and copies ran while one was open for 3% of the time, Pallas kernels for 0%

commit v1 on v0

--- a/solution.py
+++ b/solution.py
@@ -7,6 +7,12 @@
 LEN = 512
 epsilon = 1e-05
 masked_fill = -1000000000.0
+
+
+def in_order(parts, dim):
+    shape = list(parts.shape[1:])
+    shape[dim] *= parts.shape[0]
+    return jnp.moveaxis(parts, 0, dim).reshape(shape)
 
 
 def over_rows(left, right):
@@ -145,7 +151,20 @@
     sums_one = lax.psum((jnp.sum(z_one, axis=1), jnp.sum(z_one * z_one, axis=1)), "tensor")
     n_one, inv_one = norm_from(z_one, sums_one, model_width)
     h_one = n_one * gain_one.astype(jnp.float32) + bias_one.astype(jnp.float32)
-    h_low = lax.all_gather(h_one.astype(jnp.bfloat16), "tensor", axis=1, tiled=True)
+    value = h_one.astype(jnp.bfloat16)
+    size = lax.axis_size("tensor")
+    pairs = [(i, (i + 1) % size) for i in range(size)]
+    back = [(b, a) for a, b in pairs]
+    lower, upper = ([], [])
+    for step in range(size - 1):
+        if step % 2 == 0:
+            lower.append(lax.ppermute(lower[-1] if lower else value, "tensor", pairs))
+        else:
+            upper.append(lax.ppermute(upper[-1] if upper else value, "tensor", back))
+    blocks = jnp.stack([*lower[::-1], value, *upper])
+    shift = lax.axis_index("tensor") - len(lower)
+    blocks = blocks[(jnp.arange(size) - shift) % size]
+    h_low = in_order(blocks, 1)
     pre_act = jnp.dot(h_low, w_in, preferred_element_type=jnp.float32) + b_in.astype(jnp.float32)
     hidden = jax.nn.gelu(pre_act, approximate=False).astype(jnp.bfloat16)
     feed_mine = lax.psum_scatter(

time: 981 us -> 995 us (1.014)
    all_gather x1 -> x0, waiting for transfers between devices: 29.6 us -> none  [local(): lax.all_gather(h_one.astype(jnp.bfloat16), 'tensor', axis=1, tiled=True)]
    ppermute x0 -> x3, waiting for transfers between devices: none -> 26.7 us  [the longest x2 26.7 us: local(): lower.append(lax.ppermute(lower[-1] if lower else value, 'tensor', pairs))]
  transfers between devices with their start and end apart: 9 -> 11, of which waited for: 8 -> 9; matrix products, arithmetic and copies ran while one was open for 3% -> 3% of each run, Pallas kernels for 0% -> 0%
where the time goes in v1:
time: 995 us; the launch traced here: 985 us
  waiting for transfers between devices  661 us (66%)
  matrix products  114 us (11%)
  blocking collectives  78.5 us (8%)
  local copies, waits for them, and re-layouts  72.9 us (7%)
  other arithmetic  40.8 us (4%)
  between operations  14.7 us (1%)
    psum x1, waiting for transfers between devices, summed(): return lax.psum(parts, 'dp')  375 us
    reduce_scatter x1, waiting for transfers between devices, local(): lax.psum_scatter(jnp.dot(hidden, w_down, preferred_element_type=jnp.float...  58.2 us
    reduce_scatter x1, waiting for transfers between devices, local(): lax.psum_scatter(against(dpre, w_in), 'tensor', scatter_dimension=1, tile...  58 us
    reduce_scatter x1, waiting for transfers between devices, local(): lax.psum_scatter(jnp.dot(context, w_out, preferred_element_type=jnp.float...  57.4 us
    psum x1, blocking collectives, summed(): return lax.psum(parts, 'dp')  37.7 us
    unnamed x80, local copies, waits for them, and re-layouts  31.3 us
    all_gather x1, waiting for transfers between devices, local(): lax.all_gather(dz_two.astype(jnp.bfloat16), 'tensor', axis=1, tiled=True)  29.4 us
    all_gather x1, waiting for transfers between devices, local(): lax.all_gather(dz_one.astype(jnp.bfloat16), 'tensor', axis=1, tiled=True)  29.2 us
  transfers between devices with their start and end apart: 11, of which 9 were waited for; matrix products, arithmetic and copies ran while one was open for 3% of the time, Pallas kernels for 0%

profile of v1, /device:TPU:0, one launch (start us, length us, event | category | flops | bytes accessed | tf_op | source)
XLA Modules:
  0.0 984.9 jit_solution(14496282035718630677)
XLA Ops:
  14.8 26.5 %all-gather.4.cloned.1.call-done = bf16[1536,1024]{1,0:T(8,128)(2,1)} async-done(((bf16[1536,256]{1,0:T(8,128)(2,1)}), bf16[1536,1024]{1,0:T(8,128)(2,1)}) %all-gather.4.cloned.1.call-update) | async-done | bytes 3145744 | tf_op jit(solution)/shard_map/all_gather | solution.py:130
  41.2 5.2 fusion.69
  50.4 3.6 reshape.279
  56.3 3.6 reshape.277
  63.1 18.4 %while.26 = (s32[]{:T(128)}, bf16[3,512,4,64]{1,3,2,0:T(8,128)(2,1)}, f32[3,4,512]{2,1,0:T(4,128)S(1)}, bf16[3,512,4,64]{1,3,2,0:T(8,128)(2,1)}, s32[3,512]{1,0:...) while((s32[]{:T(128)}, ...), condition=%wide.region_3.4_spmd, body=%wide.region_0.3_spmd.sunk | while | flops 282196480 | bytes 14756965 | solution.py:142
  66.2 3.0 fusion.143
  72.3 3.0 fusion.143
  78.4 3.0 fusion.143
  84.5 3.7 fusion.88
  88.9 57.4 %reduce-scatter.5.cloned.1.call-done = f32[1536,256]{1,0:T(8,128)} async-done(((f32[1536,1024]{1,0:T(8,128)}), f32[1536,256]{1,0:T(8,128)}) %reduce-scatter.5.cloned.1.call-update) | async-done | bytes 1572880 | tf_op jit(solution)/shard_map/reduce_scatter | solution.py:144
  146.3 3.0 fusion.81
  149.3 10.4 %all-reduce.5 = (f32[1536]{0:T(1024)S(1)}, f32[1536]{0:T(1024)S(1)}) all-reduce(f32[1536]{0:T(1024)S(1)} %get-tuple-element.191, f32[1536]{0:T(1024)S(1)} %get-tuple-element.190), channel_id=1, replica_groups=mesh['dp'=8,'tensor'=4] {'tensor'}, use_global_device_ids=true, to_apply=%region_8.9 | all-reduce | flops 3072 | bytes 24576 | tf_op jit(solution)/shard_map/psum | solution.py:151
  159.6 2.8 fusion.77
  164.2 16.9 %collective-permute-done = bf16[1536,256]{1,0:T(8,128)(2,1)} collective-permute-done((bf16[1536,256]{1,0:T(8,128)(2,1)}, bf16[1536,256]{1,0:T(8,128)(2,1)}, u32[]{:S(2)}, u32[]{:S(2)}) %collective-permute-start) | collective-permute-done | bytes 786464 | tf_op jit(solution)/shard_map/ppermute | solution.py:161
  183.0 9.8 collective-permute-done.1
  192.8 3.1 pad_maximum_fusion
  195.9 4.3 gather_fusion
  200.2 4.7 copy.57
  204.9 19.7 %multiply_convert_fusion.1 = (bf16[1536,1024]{1,0:T(8,128)(2,1)S(1)}, f32[1536,1024]{1,0:T(8,128)}, f32[1536,1024]{1,0:T(8,128)}) fusion(f32[1024]{0:T(1024)S(1)} %convert_element_type.124, bf16[1536,1024]{0,1:T(8,128)(2,1)} %bitcast.180, bf16[1024,1024]{1,0:T(8,128)(2,1)S(1)} %copy-done), kind=kOutput, calls=%fused_computation.77 | convolution fusion | flops 3325034496 | bytes 20975616 | tf_op jit(solution)/shard_map/dot_general | solution.py:168
  226.3 5.3 fusion.89
  232.3 58.2 %reduce-scatter.7.cloned.1.call-done = f32[1536,256]{1,0:T(8,128)} async-done(((f32[1536,1024]{1,0:T(8,128)}), f32[1536,256]{1,0:T(8,128)}) %reduce-scatter.7.cloned.1.call-update) | async-done | bytes 1572880 | tf_op jit(solution)/shard_map/reduce_scatter | solution.py:170
  290.4 3.5 fusion.80
  294.0 10.1 %all-reduce.4 = (f32[1536]{0:T(1024)S(1)}, f32[1536]{0:T(1024)S(1)}) all-reduce(f32[1536]{0:T(1024)S(1)} %get-tuple-element.189, f32[1536]{0:T(1024)S(1)} %get-tuple-element.188), channel_id=1, replica_groups=mesh['dp'=8,'tensor'=4] {'tensor'}, use_global_device_ids=true, to_apply=%region_13.14 | all-reduce | flops 3072 | bytes 24576 | tf_op jit(solution)/shard_map/psum | solution.py:177
  304.1 2.6 fusion.76
  306.7 10.1 %all-reduce.3 = (f32[1536]{0:T(1024)S(1)}, f32[1536]{0:T(1024)S(1)}) all-reduce(f32[1536]{0:T(1024)S(1)} %get-tuple-element.185, f32[1536]{0:T(1024)S(1)} %get-tuple-element.192), channel_id=1, replica_groups=mesh['dp'=8,'tensor'=4] {'tensor'}, use_global_device_ids=true, to_apply=%region_17.18 | all-reduce | flops 3072 | bytes 24576 | tf_op jit(solution)/shard_map/psum | solution.py:186
  316.9 3.1 fusion.82
  322.4 29.4 %all-gather.6.cloned.1.call-done = bf16[1536,1024]{1,0:T(8,128)(2,1)} async-done(((bf16[1536,256]{1,0:T(8,128)(2,1)}), bf16[1536,1024]{1,0:T(8,128)(2,1)}) %all-gather.6.cloned.1.call-update) | async-done | bytes 3145744 | tf_op jit(solution)/shard_map/all_gather | solution.py:191
  351.7 11.8 %convert_reduce_fusion = (f32[1024]{0:T(1024)S(1)}, bf16[1536,1024]{1,0:T(8,128)(2,1)S(1)}) fusion(f32[1536,1024]{1,0:T(8,128)} %get-tuple-element.260, f32[1536,1024]{1,0:T(8,128)} %get-tuple-element.277, f32[1024]{0:T(1024)S(1)} %convert_element_type.124, bf16[1536,1024]{1,0:T(8,128)(2,1)} %all-gather.6.cloned.1.call-done, bf16[1024,1024]{1,0:T(8,128)(2,1)} %param.35), kind=kOutput, calls=%fused_computation.75 | convolution fusion | flops 3247963136 | bytes 20979712 | tf_op jit(solution)/shard_map/dot_general | solution.py:25
  365.2 5.6 fusion.90
  370.9 58.0 %reduce-scatter.9.cloned.1.call-done = f32[1536,256]{1,0:T(8,128)} async-done(((f32[1536,1024]{1,0:T(8,128)}), f32[1536,256]{1,0:T(8,128)}) %reduce-scatter.9.cloned.1.call-update) | async-done | bytes 1572880 | tf_op jit(solution)/shard_map/reduce_scatter | solution.py:198
  428.9 3.4 multiply_reduce_fusion.1
  432.3 10.1 %all-reduce.2 = (f32[1536]{0:T(1024)S(1)}, f32[1536]{0:T(1024)S(1)}) all-reduce(f32[1536]{0:T(1024)S(1)} %get-tuple-element.183, f32[1536]{0:T(1024)S(1)} %get-tuple-element.186), channel_id=1, replica_groups=mesh['dp'=8,'tensor'=4] {'tensor'}, use_global_device_ids=true, to_apply=%region_22.23 | all-reduce | flops 3072 | bytes 24576 | tf_op jit(solution)/shard_map/psum | solution.py:205
  447.3 29.2 %all-gather.8.cloned.1.call-done = bf16[1536,1024]{1,0:T(8,128)(2,1)} async-done(((bf16[1536,256]{1,0:T(8,128)(2,1)}), bf16[1536,1024]{1,0:T(8,128)(2,1)}) %all-gather.8.cloned.1.call-update) | async-done | bytes 3145744 | tf_op jit(solution)/shard_map/all_gather | solution.py:210
  476.5 2.9 convolution_convert_fusion.1
  481.0 3.4 copy.61
  486.4 26.4 %while.27 = (s32[]{:T(128)}, bf16[3,512,4,64]{1,3,2,0:T(8,128)(2,1)}, bf16[3,512,4,64]{1,3,2,0:T(8,128)(2,1)}, bf16[3,512,4,64]{1,3,2,0:T(8,128)(2,1)S(1)}, bf16...) while((s32[]{:T(128)}, ...), condition=%wide.region_25.26_spmd, body=%wide.region_23.25_spmd.sunk | while | flops 688519680 | bytes 38344856 | solution.py:213
  488.7 2.5 multiply_reduce_fusion.7
  497.5 2.5 multiply_reduce_fusion.7
  506.3 2.5 multiply_reduce_fusion.7
  518.5 5.4 convolution_convert_fusion
  524.2 8.6 fusion.92
  532.8 5.0 fusion.93
  537.8 2.6 convolution_bitcast_fusion
  548.5 37.7 %all-reduce = (f32[256]{0:T(256)}, f32[256]{0:T(256)}, f32[256]{0:T(256)}, f32[256]{0:T(256)}, f32[256]{0:T(256)}, /*index=5*/f32[1024]{0:T(1024)}, f32[256]{0:T(256)}, f32[256]{0:T(256)}, f32[256]{0:T(256)}) all-reduce(f32[256]{0:T(256)S(1)} %reduce_sum.184, f32[256]{0:T(256)S(1)} %reduce_sum.186, ...), channel_id=1, replica_groups=mesh['dp'=8,'tensor'=4] {'dp'}, use_global_device_ids=true, to_apply=%region_31.32 | all-reduce | flops 3072 | bytes 24576 | tf_op jit(solution)/shard_map/psum | solution.py:94
  588.4 375.1 %all-reduce.8.cloned.1.call-done = (f32[1024,256]{0,1:T(8,128)}, f32[1024,256]{0,1:T(8,128)}, f32[1024,256]{0,1:T(8,128)}, f32[256,1024]{1,0:T(8,128)}, f32[1024,1024]{1,0:T(8,128)}, /*index=5*/f32[1024,1024]{1,0:T(8,128)}) async-done(((f32[1024,256]{0,1:T(8,128)}, f32[1024,256]{0,1:T(8,128)}, f32[1024,256]{0,1:T(8,128)}, f32[256,1024]{1,0:T(8,128)}, f32[1024,1024]{1,0:T(8,128)}, ...) | async-done | bytes 12582928 | tf_op jit(solution)/shard_map/psum | solution.py:94
  963.4 2.7 copy.66
  966.1 2.5 copy.67
  970.9 4.9 copy.118
  (194 shorter events, 87.7 us)
Async XLA Ops:
  7.2 197.7 %copy-start = (bf16[1024,1024]{1,0:T(8,128)(2,1)S(1)}, bf16[1024,1024]{1,0:T(8,128)(2,1)}, u32[]{:S(2)}) copy-start(bf16[1024,1024]{1,0:T(8,128)(2,1)} %param.33) | copy-start | bytes 6291460
  7.2 6.7 copy-start.17
  7.2 34.0 %all-gather.4.cloned.1.call-start = ((), (), s32[]{:S(2)}) async-start(), calls=%async_computation.4 | async-start | bytes 3932160 | tf_op jit(solution)/shard_map/all_gather | solution.py:130
  8.0 138.3 %reduce-scatter.5.cloned.1.call-start = ((), (), s32[]{:S(2)}) async-start(), calls=%async_computation.5 | async-start | bytes 7864320 | tf_op jit(solution)/shard_map/reduce_scatter | solution.py:144
  81.5 3.0 copy-start.16
  83.6 0.9 copy-start.10
  88.2 0.7 copy-start.25
  88.2 0.7 copy-start.26
  88.2 0.7 copy-start.27
  88.3 202.2 %reduce-scatter.7.cloned.1.call-start = ((), (), s32[]{:S(2)}) async-start(), calls=%async_computation.6 | async-start | bytes 7864320 | tf_op jit(solution)/shard_map/reduce_scatter | solution.py:170
  88.9 92.2 %copy-start.20 = (bf16[1024]{0:T(1024)(128)(2,1)S(1)}, bf16[1024]{0:T(1024)(128)(2,1)}, u32[]{:S(2)}) copy-start(bf16[1024]{0:T(1024)(128)(2,1)} %param.34) | copy-start | bytes 6148
  162.4 18.7 %collective-permute-start = (bf16[1536,256]{1,0:T(8,128)(2,1)}, bf16[1536,256]{1,0:T(8,128)(2,1)}, u32[]{:S(2)}, u32[]{:S(2)}) collective-permute-start(bf16[1536,256]{1,0:T(8,128)(2,1)} %fusion.77), channel_id=1, source_target_pairs={{0,1},{1,2},{2,3},{3,0},{4,5},{5,6},{6,7},{7,4},{8,9},{9,10},{10,1... | collective-permute-start | bytes 2359304 | tf_op jit(solution)/shard_map/ppermute | solution.py:161
  162.4 20.6 %collective-permute-start.2 = (bf16[1536,256]{1,0:T(8,128)(2,1)}, bf16[1536,256]{1,0:T(8,128)(2,1)}, u32[]{:S(2)}, u32[]{:S(2)}) collective-permute-start(bf16[1536,256]{1,0:T(8,128)(2,1)} %fusion.77), channel_id=1, source_target_pairs={{1,0},{2,1},{3,2},{0,3},{5,4},{6,5},{7,6},{4,7},{9,8},{10,9},{11,1... | collective-permute-start | bytes 2359304 | tf_op jit(solution)/shard_map/ppermute | solution.py:163
  181.1 11.7 %collective-permute-start.1 = (bf16[1536,256]{1,0:T(8,128)(2,1)}, bf16[1536,256]{1,0:T(8,128)(2,1)}, u32[]{:S(2)}, u32[]{:S(2)}) collective-permute-start(bf16[1536,256]{1,0:T(8,128)(2,1)} %collective-permute-done), channel_id=1, source_target_pairs={{0,1},{1,2},{2,3},{3,0},{4,5},{5,6},{6,7},{7,4},{8,9},{9,10},{10,1... | collective-permute-start | bytes 2359304 | tf_op jit(solution)/shard_map/ppermute | solution.py:161
  204.9 21.4 %copy-start.24 = (bf16[1024,1024]{1,0:T(8,128)(2,1)S(1)}, bf16[1024,1024]{1,0:T(8,128)(2,1)}, u32[]{:S(2)}) copy-start(bf16[1024,1024]{1,0:T(8,128)(2,1)} %param.35) | copy-start | bytes 6291460
  224.5 1.8 copy-start.31
  231.6 0.7 copy-start.28
  231.6 0.7 copy-start.29
  231.6 0.7 copy-start.30
  231.6 120.1 %all-gather.6.cloned.1.call-start = ((), (), s32[]{:S(2)}) async-start(), calls=%async_computation.7 | async-start | bytes 3932160 | tf_op jit(solution)/shard_map/all_gather | solution.py:191
  320.0 1.1 copy-start.6
  322.1 106.8 %reduce-scatter.9.cloned.1.call-start = ((), (), s32[]{:S(2)}) async-start(), calls=%async_computation.8 | async-start | bytes 7864320 | tf_op jit(solution)/shard_map/reduce_scatter | solution.py:198
  363.6 1.7 copy-start.33
  370.8 58.1 %copy-start.2 = (f32[1536,256]{1,0:T(8,128)S(1)}, f32[1536,256]{1,0:T(8,128)}, u32[]{:S(2)}) copy-start(f32[1536,256]{1,0:T(8,128)} %get-tuple-element.261) | copy-start | bytes 4718596
  370.8 105.7 %all-gather.8.cloned.1.call-start = ((), (), s32[]{:S(2)}) async-start(), calls=%async_computation.9 | async-start | bytes 3932160 | tf_op jit(solution)/shard_map/all_gather | solution.py:210
  444.7 1.2 copy-start.4
  446.9 139.3 %reduce-scatter.11.cloned.1.call-start = ((), (), s32[]{:S(2)}) async-start(), calls=%async_computation.10 | async-start | bytes 3932160 | tf_op jit(solution)/shard_map/reduce_scatter | solution.py:227
  479.4 6.9 copy-start.3
  486.4 1.1 copy-start.9
  495.1 1.1 copy-start.9
  503.9 1.1 copy-start.9
  512.7 3.2 copy-start.7
  514.8 1.2 copy-start.13
  517.1 1.4 copy-start.18
  523.9 439.5 %all-reduce.8.cloned.1.call-start = ((), (), s32[]{:S(2)}) async-start(), calls=%async_computation.11 | async-start | bytes 25165824 | tf_op jit(solution)/shard_map/psum | solution.py:94
  524.2 8.6 copy-start.22
  524.2 8.6 copy-start.32
  532.8 5.0 copy-start.19
  532.8 5.0 copy-start.21
  540.4 1.8 copy-start.11
  540.4 3.3 copy-start.23
  545.7 1.1 copy-start.8
  545.7 40.4 %copy-start.5 = (f32[1536,256]{1,0:T(8,128)S(1)}, f32[1536,256]{1,0:T(8,128)}, u32[]{:S(2)}) copy-start(f32[1536,256]{1,0:T(8,128)} %copy-done.4) | copy-start | bytes 4718596
  963.4 5.2 copy-start.15
  963.4 6.5 copy-start.14
  970.9 4.9 copy-start.12
  970.9 7.0 copy-start.1
Sparse Core Ops, SparseCore 0:
  9.6 31.6 all-gather.3
  88.4 57.8 reduce-scatter.4
  231.7 58.6 reduce-scatter.6
  322.2 29.4 all-gather.5
  371.0 57.8 reduce-scatter.8
  447.0 29.4 all-gather.7
  524.1 37.7 reduce-scatter.10
  568.4 395.0 all-reduce.7
